TPU v7x, 32 devices: a whole 2x2x4 slice. The times are simulated.
32 devices in a mesh: dp: 2 (over core), seq: 8 (over z, x), mp: 2 (over y).
Axes of the slice: x: 2, y: 2, z: 4, core: 2. Of those that a mesh axis runs over, the one named last changes fastest.
Arguments:
- queries: bfloat16 [4, 1024, 4096], P('dp', 'seq', 'mp'), may hold values from -6 to 6
- vision: bfloat16 [4, 640, 4096], P('dp', 'seq'), may hold values from -6 to 6
- key_weight: bfloat16 [4096, 1024], P(None, 'mp'), may hold values from -0.09375 to 0.09375
- value_weight: bfloat16 [4096, 1024], P(None, 'mp'), may hold values from -0.09375 to 0.09375
- query_gain: float32 [128], replicated, may hold values from 0.6 to 6
- key_gain: float32 [128], replicated, may hold values from 0.6 to 6
- out_grad: bfloat16 [4, 1024, 4096], P('dp', 'seq', 'mp'), may hold values from -6 to 6
- tile_count: int32 [4], P('dp'), may hold values from 1 to 4, as said below
Outputs:
- query_grad: bfloat16 [4, 1024, 4096], P('dp', 'seq', 'mp')
- vision_grad: bfloat16 [4, 640, 4096], P('dp', 'seq', 'mp')
- key_weight_grad: float32 [4096, 1024], P(None, 'mp')
- value_weight_grad: float32 [4096, 1024], P(None, 'mp')
Inputs may be any that keep to these rules, and one draw needn't show every extreme that they name: The live vision tokens of sample s are its first tile_count[s] * 160; some sample has 4 tiles and some other sample has 1.
All inputs are finite; a program needn't handle non-finite values.
Results may differ from a plain program's by a relative error of at most 0.03.
The roundings to bfloat16 on the way count: a program that leaves them out, or rounds other values in their place, can miss the bound.
Values may be sent and summed in bfloat16 or wider, within the bound.
A program may use at most 128 MiB of HBM per device.

v0:
```python
import jax
import jax.numpy as jnp
from jax import lax
from jax.sharding import PartitionSpec as P

MAX_TILES = 4
EPS = 1e-05
NEG = -1e30


def norm_apply(raw, gain):
    inverse = lax.rsqrt(jnp.mean(raw * raw, axis=-1, keepdims=True) + EPS)
    return (raw * inverse * gain, inverse)


def norm_back(raw, inverse, gain, upstream):
    weighted = upstream * gain
    return inverse * weighted - raw * inverse * inverse * inverse * jnp.mean(
        weighted * raw, axis=-1, keepdims=True
    )


def sample_grads(normed, out_heads, keys_all, values_all, tiles_here, score_scale):
    text_rows, kv_here, group_size, head_dim = normed.shape
    block_len = keys_all.shape[0] // MAX_TILES
    stat_shape = (kv_here, group_size, text_rows, 1)

    def scores_of(block_at):
        key_block = keys_all[block_at * block_len : (block_at + 1) * block_len]
        return (
            jnp.einsum("tkgd,jkd->kgtj", normed, key_block, preferred_element_type=jnp.float32)
            * score_scale
        )

    row_max = jnp.full(stat_shape, NEG, jnp.float32)
    row_sum = jnp.zeros(stat_shape, jnp.float32)
    for block_at in range(MAX_TILES):
        live_flag = block_at < tiles_here

        def update_stats(carry, block_at=block_at, live_flag=live_flag):
            old_max, old_sum = carry
            scores = jnp.where(live_flag, scores_of(block_at), NEG)
            new_max = jnp.maximum(old_max, jnp.max(scores, axis=-1, keepdims=True))
            new_sum = old_sum * jnp.exp(old_max - new_max) + jnp.sum(
                jnp.exp(scores - new_max), axis=-1, keepdims=True
            )
            return (new_max, new_sum)

        row_max, row_sum = update_stats((row_max, row_sum))

    def probs_of(block_at, live_flag):
        scores = scores_of(block_at)
        return jnp.where(live_flag, jnp.exp(scores - row_max) / row_sum, 0.0)

    attn_total = jnp.zeros((text_rows, kv_here, group_size, head_dim), jnp.float32)
    value_part = jnp.zeros((keys_all.shape[0], kv_here, head_dim), jnp.float32)
    for block_at in range(MAX_TILES):
        live_flag = block_at < tiles_here

        def forward_block(carry, block_at=block_at, live_flag=live_flag):
            attn_now, value_now = carry
            probs_b = probs_of(block_at, live_flag).astype(jnp.bfloat16)
            value_block = values_all[block_at * block_len : (block_at + 1) * block_len]
            attn_now = attn_now + jnp.einsum(
                "kgtj,jkd->tkgd", probs_b, value_block, preferred_element_type=jnp.float32
            )
            block_grad = jnp.einsum(
                "kgtj,tkgd->jkd", probs_b, out_heads, preferred_element_type=jnp.float32
            )
            value_now = value_now.at[block_at * block_len : (block_at + 1) * block_len].set(
                block_grad
            )
            return (attn_now, value_now)

        attn_total, value_part = forward_block((attn_total, value_part))
    attn_b = attn_total.astype(jnp.bfloat16)
    delta = jnp.sum(out_heads.astype(jnp.float32) * attn_b.astype(jnp.float32), axis=-1)
    delta = delta.transpose(1, 2, 0)[..., None]
    dnormed = jnp.zeros((text_rows, kv_here, group_size, head_dim), jnp.float32)
    key_part = jnp.zeros((keys_all.shape[0], kv_here, head_dim), jnp.float32)
    for block_at in range(MAX_TILES):
        live_flag = block_at < tiles_here

        def backward_block(carry, block_at=block_at, live_flag=live_flag):
            query_now, key_now = carry
            probs = probs_of(block_at, live_flag)
            key_block = keys_all[block_at * block_len : (block_at + 1) * block_len]
            value_block = values_all[block_at * block_len : (block_at + 1) * block_len]
            dprobs = jnp.einsum(
                "tkgd,jkd->kgtj", out_heads, value_block, preferred_element_type=jnp.float32
            )
            dscores = (probs * (dprobs - delta)).astype(jnp.bfloat16)
            query_now = query_now + jnp.einsum(
                "kgtj,jkd->tkgd", dscores, key_block, preferred_element_type=jnp.float32
            )
            block_grad = (
                jnp.einsum("kgtj,tkgd->jkd", dscores, normed, preferred_element_type=jnp.float32)
                * score_scale
            )
            key_now = key_now.at[block_at * block_len : (block_at + 1) * block_len].set(block_grad)
            return (query_now, key_now)

        dnormed, key_part = backward_block((dnormed, key_part))
    return (dnormed * score_scale, key_part, value_part)


def local(queries, vision, key_weight, value_weight, query_gain, key_gain, out_grad, tile_count):
    head_dim = query_gain.shape[0]
    samples_here, vision_rows, model_width = vision.shape
    text_rows = queries.shape[1]
    kv_here = key_weight.shape[1] // head_dim
    group_size = queries.shape[2] // head_dim // kv_here
    score_scale = head_dim ** (-0.5)
    flat_vision = vision.reshape(samples_here * vision_rows, model_width)
    key_raw = jnp.dot(flat_vision, key_weight, preferred_element_type=jnp.float32)
    key_raw = key_raw.reshape(samples_here, vision_rows, kv_here, head_dim)
    key_normed, key_inverse = norm_apply(key_raw, key_gain)
    own_keys = key_normed.astype(jnp.bfloat16)
    own_values = jnp.dot(flat_vision, value_weight, preferred_element_type=jnp.float32).astype(
        jnp.bfloat16
    )
    own_values = own_values.reshape(samples_here, vision_rows, kv_here, head_dim)
    keys_all, values_all = (
        lax.all_gather(own_keys, "seq", axis=1, tiled=True),
        lax.all_gather(own_values, "seq", axis=1, tiled=True),
    )
    query_raw = queries.astype(jnp.float32).reshape(
        samples_here, text_rows, kv_here, group_size, head_dim
    )
    query_normed, query_inverse = norm_apply(query_raw, query_gain)
    normed = query_normed.astype(jnp.bfloat16)
    out_heads = out_grad.reshape(samples_here, text_rows, kv_here, group_size, head_dim)
    query_list = []
    key_list = []
    value_list = []
    for sample_at in range(samples_here):
        query_part, key_part, value_part = sample_grads(
            normed[sample_at],
            out_heads[sample_at],
            keys_all[sample_at],
            values_all[sample_at],
            tile_count[sample_at],
            score_scale,
        )
        query_list.append(query_part)
        key_list.append(key_part)
        value_list.append(value_part)
    key_sum, value_sum = (
        lax.psum_scatter(
            jnp.stack(key_list).astype(jnp.bfloat16), "seq", scatter_dimension=1, tiled=True
        ).astype(jnp.float32),
        lax.psum_scatter(
            jnp.stack(value_list).astype(jnp.bfloat16), "seq", scatter_dimension=1, tiled=True
        ).astype(jnp.float32),
    )
    key_grad = norm_back(key_raw, key_inverse, key_gain, key_sum).astype(jnp.bfloat16)
    value_grad = value_sum.astype(jnp.bfloat16)
    query_grad = norm_back(query_raw, query_inverse, query_gain, jnp.stack(query_list))
    query_grad = query_grad.astype(jnp.bfloat16).reshape(queries.shape)
    key_flat = key_grad.reshape(samples_here * vision_rows, kv_here * head_dim)
    value_flat = value_grad.reshape(samples_here * vision_rows, kv_here * head_dim)
    heads_key, heads_value = (
        lax.all_gather(key_grad, "mp", axis=2, tiled=True),
        lax.all_gather(value_grad, "mp", axis=2, tiled=True),
    )
    rows_key, rows_value = (
        lax.all_to_all(key_weight, "mp", split_axis=0, concat_axis=1, tiled=True),
        lax.all_to_all(value_weight, "mp", split_axis=0, concat_axis=1, tiled=True),
    )
    every_head = heads_key.shape[2] * head_dim
    vision_part = jnp.einsum(
        "rc,dc->rd",
        heads_key.reshape(samples_here * vision_rows, every_head),
        rows_key,
        preferred_element_type=jnp.float32,
    )
    vision_part = vision_part + jnp.einsum(
        "rc,dc->rd",
        heads_value.reshape(samples_here * vision_rows, every_head),
        rows_value,
        preferred_element_type=jnp.float32,
    )
    vision_grad = vision_part.astype(jnp.bfloat16).reshape(
        samples_here, vision_rows, vision_part.shape[1]
    )
    key_weight_local = jnp.einsum(
        "rd,rc->dc", flat_vision, key_flat, preferred_element_type=jnp.float32
    )
    value_weight_local = jnp.einsum(
        "rd,rc->dc", flat_vision, value_flat, preferred_element_type=jnp.float32
    )
    key_weight_grad, value_weight_grad = (
        lax.psum(key_weight_local.astype(jnp.bfloat16), ("dp", "seq")).astype(jnp.float32),
        lax.psum(value_weight_local.astype(jnp.bfloat16), ("dp", "seq")).astype(jnp.float32),
    )
    return (query_grad, vision_grad, key_weight_grad, value_weight_grad)


def solution(mesh):
    in_specs = (
        P("dp", "seq", "mp"),
        P("dp", "seq", None),
        P(None, "mp"),
        P(None, "mp"),
        P(),
        P(),
        P("dp", "seq", "mp"),
        P("dp"),
    )
    out_specs = (P("dp", "seq", "mp"), P("dp", "seq", "mp"), P(None, "mp"), P(None, "mp"))
    return jax.shard_map(local, mesh=mesh, in_specs=in_specs, out_specs=out_specs, check_vma=False)
```

profile of v0, /device:TPU:0, one launch (start us, length us, event | category | flops | bytes accessed | tf_op | source)
XLA Modules:
  0.0 458.0 jit_solution(17486867492207146060)
XLA Ops:
  7.2 6.4 %copy.174 = bf16[512,4096]{1,0:T(8,128)(2,1)} copy(bf16[512,4096]{0,1:T(8,128)(2,1)} %bitcast.564) | data formatting | bytes 8388608 | tf_op jit(solution)/shard_map/dot_general | solution.py:115
  13.6 3.9 multiply_reduce_fusion.2
  18.4 5.6 %all-to-all-start.1 = ((bf16[2,2048,512]{2,1,0:T(8,128)(2,1)}), bf16[2,2048,512]{2,1,0:T(8,128)(2,1)}, u32[]{:S(2)}, u32[]{:S(2)}) async-start(bf16[2,2048,512]{2,1,0:T(8,128)(2,1)} %bitcast.563), calls=%async_computation.3 | async-start | bytes 8388608 | tf_op jit(solution)/shard_map/all_to_all | solution.py:168
  24.1 3.0 convolution_convert_fusion.2
  33.8 1.6 copy.74
  35.4 2.5 fusion.117
  37.9 2.1 copy.175
  41.0 1.6 multiply_reduce_fusion
  42.6 3.0 copy.77
  45.6 2.2 multiply_convert_fusion
  47.8 16.0 %all-gather.3.cloned.1.call-done = bf16[2,640,4,128]{3,1,2,0:T(8,128)(2,1)} async-done(((bf16[2,80,4,128]{3,1,2,0:T(8,128)(2,1)}), bf16[2,640,4,128]{3,1,2,0:T(8,128)(2,1)}) %all-gather.3.cloned.1.call-update) | async-done | bytes 1310736 | tf_op jit(solution)/shard_map/all_gather | solution.py:124
  63.8 1.3 select_reduce_fusion
  65.1 1.5 select_reduce_fusion.1
  66.6 1.5 select_reduce_fusion.2
  68.1 1.5 select_reduce_fusion.3
  71.6 36.1 %all-gather.5.cloned.1.call-done = bf16[2,640,4,128]{3,1,2,0:T(8,128)(2,1)} async-done(((bf16[2,80,4,128]{3,1,2,0:T(8,128)(2,1)}), bf16[2,640,4,128]{3,1,2,0:T(8,128)(2,1)}) %all-gather.5.cloned.1.call-update) | async-done | bytes 1310736 | tf_op jit(solution)/shard_map/all_gather | solution.py:125
  107.6 1.9 fusion.94
  127.6 1.2 pad_maximum_fusion
  129.8 1.8 convolution_bitcast_fusion.23
  138.7 1.2 pad_maximum_fusion.1
  139.9 5.6 %all-to-all-start = ((bf16[2,2048,512]{2,1,0:T(8,128)(2,1)}), bf16[2,2048,512]{2,1,0:T(8,128)(2,1)}, u32[]{:S(2)}, u32[]{:S(2)}) async-start(bf16[2,2048,512]{2,1,0:T(8,128)(2,1)} %bitcast.565), calls=%async_computation.1 | async-start | bytes 8388608 | tf_op jit(solution)/shard_map/all_to_all | solution.py:167
  145.6 47.1 %reduce-scatter.3.cloned.1.call-done = bf16[2,80,4,128]{3,1,2,0:T(8,128)(2,1)} async-done(((bf16[2,640,4,128]{3,1,2,0:T(8,128)(2,1)}), bf16[2,80,4,128]{3,1,2,0:T(8,128)(2,1)}) %reduce-scatter.3.cloned.1.call-update) | async-done | bytes 163856 | tf_op jit(solution)/shard_map/reduce_scatter | solution.py:149
  192.8 1.1 multiply_reduce_fusion.1
  193.9 1.2 subtract_convert_fusion
  195.8 64.9 %reduce-scatter.5.cloned.1.call-done = bf16[2,80,4,128]{3,1,2,0:T(8,128)(2,1)} async-done(((bf16[2,640,4,128]{3,1,2,0:T(8,128)(2,1)}), bf16[2,80,4,128]{3,1,2,0:T(8,128)(2,1)}) %reduce-scatter.5.cloned.1.call-update) | async-done | bytes 163856 | tf_op jit(solution)/shard_map/reduce_scatter | solution.py:152
  261.7 3.2 fusion
  264.9 3.2 fusion.1
  268.2 6.6 %copy.111 = bf16[2048,2,512]{0,2,1:T(8,128)(2,1)} copy(bf16[2048,2,512]{2,0,1:T(8,128)(2,1)} %bitcast.180) | data formatting | bytes 8388608 | tf_op jit(solution)/shard_map/all_to_all | solution.py:168
  274.9 6.2 %copy.101 = bf16[2048,2,512]{0,2,1:T(8,128)(2,1)} copy(bf16[2048,2,512]{2,0,1:T(8,128)(2,1)} %bitcast.145) | data formatting | bytes 8388608 | tf_op jit(solution)/shard_map/all_to_all | solution.py:167
  281.1 1.5 fusion.110
  282.6 1.5 convolution_add_fusion.3
  284.1 1.5 convolution_add_fusion.2
  285.7 1.5 fusion.32
  287.2 1.3 copy.98
  288.7 1.5 fusion.109
  290.3 1.5 convolution_add_fusion.9
  291.8 1.5 convolution_add_fusion.8
  293.3 2.4 fusion.33
  295.8 2.7 copy.88
  298.5 2.4 fusion.7
  301.7 1.3 copy.114
  303.0 6.0 %all_gather.15 = bf16[2,80,8,128]{3,1,2,0:T(8,128)(2,1)S(1)} all-gather(bf16[2,80,4,128]{3,1,2,0:T(8,128)(2,1)S(1)} %copy-done.31), channel_id=1, replica_groups=mesh['dp'=2,'seq'=8,'mp'=2] {'mp'}, dimensions={2}, use_global_device_ids=true | all-gather | bytes 491520 | tf_op jit(solution)/shard_map/all_gather | solution.py:164
  309.1 6.0 %all_gather.14 = bf16[2,80,8,128]{3,1,2,0:T(8,128)(2,1)S(1)} all-gather(bf16[2,80,4,128]{3,1,2,0:T(8,128)(2,1)S(1)} %copy-done.28), channel_id=1, replica_groups=mesh['dp'=2,'seq'=8,'mp'=2] {'mp'}, dimensions={2}, use_global_device_ids=true | all-gather | bytes 491520 | tf_op jit(solution)/shard_map/all_gather | solution.py:163
  315.2 3.3 fusion.84
  318.9 1.7 fusion.2
  320.6 116.8 %all-reduce.7.cloned.1.call-done = (bf16[4096,512]{0,1:T(8,128)(2,1)}, bf16[4096,512]{0,1:T(8,128)(2,1)}) async-done(((bf16[4096,512]{0,1:T(8,128)(2,1)}, bf16[4096,512]{0,1:T(8,128)(2,1)}), (bf16[4096,512]{0,1:T(8,128)(2,1)}, bf16[4096,512]{0,1:T(8,128)(2,1)})) %all-reduce.7.cloned.1.call-update) | async-done | bytes 8388624 | tf_op jit(solution)/shard_map/psum | solution.py:193
  437.4 7.0 %copy.115 = f32[4096,512]{1,0:T(8,128)} copy(bf16[4096,512]{0,1:T(8,128)(2,1)} %get-tuple-element.208) | data formatting | bytes 12582912
  444.4 7.0 %copy.116 = f32[4096,512]{1,0:T(8,128)} copy(bf16[4096,512]{0,1:T(8,128)(2,1)} %get-tuple-element.209) | data formatting | bytes 12582912
  (185 shorter events, 34.4 us)
Async XLA Ops:
  7.2 6.5 %copy-start = (bf16[2,80,4096]{2,1,0:T(8,128)(2,1)S(1)}, bf16[2,80,4096]{2,1,0:T(8,128)(2,1)}, u32[]{:S(2)}) copy-start(bf16[2,80,4096]{2,1,0:T(8,128)(2,1)} %param.41) | copy-start | bytes 3932164
  7.2 56.7 %all-gather.3.cloned.1.call-start = ((), (), s32[]{:S(2)}) async-start(), calls=%async_computation.4 | async-start | bytes 1474560 | tf_op jit(solution)/shard_map/all_gather | solution.py:124
  13.6 3.9 copy-start.51
  18.4 121.5 %all-to-all-start.1 = ((bf16[2,2048,512]{2,1,0:T(8,128)(2,1)}), bf16[2,2048,512]{2,1,0:T(8,128)(2,1)}, u32[]{:S(2)}, u32[]{:S(2)}) async-start(bf16[2,2048,512]{2,1,0:T(8,128)(2,1)} %bitcast.563), calls=%async_computation.3 | async-start | bytes 8388608 | tf_op jit(solution)/shard_map/all_to_all | solution.py:168
  24.1 83.6 %all-gather.5.cloned.1.call-start = ((), (), s32[]{:S(2)}) async-start(), calls=%async_computation.5 | async-start | bytes 1474560 | tf_op jit(solution)/shard_map/all_gather | solution.py:125
  24.1 3.9 copy-start.54
  27.9 164.8 %reduce-scatter.3.cloned.1.call-start = ((), (), s32[]{:S(2)}) async-start(), calls=%async_computation.6 | async-start | bytes 1474560 | tf_op jit(solution)/shard_map/reduce_scatter | solution.py:149
  35.4 5.6 %copy-start.3 = (bf16[2,128,2048]{1,2,0:T(8,128)(2,1)}, bf16[2,128,2048]{1,2,0:T(8,128)(2,1)S(1)}, u32[]{:S(2)}) copy-start(bf16[2,128,2048]{1,2,0:T(8,128)(2,1)S(1)} %copy.74) | copy-start | bytes 3145732
  42.6 3.0 copy-start.52
  65.1 5.0 %copy-start.7 = (f32[4,4,128,160]{2,3,1,0:T(8,128)}, f32[4,4,128,160]{2,3,1,0:T(8,128)S(1)}, u32[]{:S(2)}) copy-start(f32[4,4,128,160]{2,3,1,0:T(8,128)S(1)} %get-tuple-element.227) | copy-start | bytes 3932164
  66.6 3.6 copy-start.10
  68.1 2.1 copy-start.13
  107.6 2.0 copy-start.14
  107.6 2.2 copy-start.55
  109.8 1.3 copy-start.11
  111.1 1.3 copy-start.8
  112.5 1.4 copy-start.47
  114.3 1.3 copy-start.6
  116.0 10.2 %copy-start.16 = (f32[4,4,128,160]{2,3,1,0:T(8,128)}, f32[4,4,128,160]{2,3,1,0:T(8,128)S(1)}, u32[]{:S(2)}) copy-start(f32[4,4,128,160]{2,3,1,0:T(8,128)S(1)} %get-tuple-element.235) | copy-start | bytes 3932164
  116.4 8.9 %copy-start.18 = (f32[4,4,128,160]{2,3,1,0:T(8,128)}, f32[4,4,128,160]{2,3,1,0:T(8,128)S(1)}, u32[]{:S(2)}) copy-start(f32[4,4,128,160]{2,3,1,0:T(8,128)S(1)} %get-tuple-element.237) | copy-start | bytes 3932164
  116.8 7.4 %copy-start.20 = (f32[4,4,128,160]{2,3,1,0:T(8,128)}, f32[4,4,128,160]{2,3,1,0:T(8,128)S(1)}, u32[]{:S(2)}) copy-start(f32[4,4,128,160]{2,3,1,0:T(8,128)S(1)} %get-tuple-element.239) | copy-start | bytes 3932164
  117.1 3.5 copy-start.22
  118.3 8.0 %copy-start.49 = (f32[4,4,128]{2,1,0:T(4,128)}, f32[4,4,128]{2,1,0:T(4,128)S(1)}, u32[]{:S(2)}) copy-start(f32[4,4,128]{2,1,0:T(4,128)S(1)} %multiply_add_fusion.1) | copy-start | bytes 24580
  128.8 131.9 %reduce-scatter.5.cloned.1.call-start = ((), (), s32[]{:S(2)}) async-start(), calls=%async_computation.7 | async-start | bytes 1474560 | tf_op jit(solution)/shard_map/reduce_scatter | solution.py:152
  129.8 1.9 copy-start.15
  129.8 1.9 copy-start.48
  131.7 1.3 copy-start.12
  134.4 1.3 copy-start.21
  134.4 1.3 copy-start.50
  135.7 1.3 copy-start.19
  139.9 134.9 %all-to-all-start = ((bf16[2,2048,512]{2,1,0:T(8,128)(2,1)}), bf16[2,2048,512]{2,1,0:T(8,128)(2,1)}, u32[]{:S(2)}, u32[]{:S(2)}) async-start(bf16[2,2048,512]{2,1,0:T(8,128)(2,1)} %bitcast.565), calls=%async_computation.1 | async-start | bytes 8388608 | tf_op jit(solution)/shard_map/all_to_all | solution.py:167
  145.6 291.8 %all-reduce.7.cloned.1.call-start = ((), (), s32[]{:S(2)}) async-start(), calls=%async_computation.8 | async-start | bytes 16777216 | tf_op jit(solution)/shard_map/psum | solution.py:193
  281.1 1.5 copy-start.39
  282.6 1.5 copy-start.41
  284.1 1.5 copy-start.43
  287.1 3.1 copy-start.5
  287.1 1.6 copy-start.30
  288.7 1.5 copy-start.35
  290.3 1.5 copy-start.37
  291.8 1.5 copy-start.33
  295.8 2.7 copy-start.1
  295.8 2.7 copy-start.53
  298.5 2.4 copy-start.4
  298.5 2.4 copy-start.25
  298.5 2.5 copy-start.26
  301.7 1.3 copy-start.31
  301.7 7.4 %copy-start.28 = (bf16[2,80,4,128]{3,1,2,0:T(8,128)(2,1)S(1)}, bf16[2,80,4,128]{3,1,2,0:T(8,128)(2,1)}, u32[]{:S(2)}) copy-start(bf16[2,80,4,128]{3,1,2,0:T(8,128)(2,1)} %copy-done.27) | copy-start | bytes 491524
  315.2 3.7 copy-start.2
  (15 other events, 15.4 us)
Sparse Core Ops, SparseCore 0:
  18.6 45.2 all-gather.2
  66.6 40.9 all-gather.4
  128.9 63.7 reduce-scatter.2
  196.6 64.0 reduce-scatter.4
  268.3 169.0 all-reduce.6
where the time goes:
time: 460 us; the launch traced here: 458 us
  waiting for transfers between devices  281 us (61%)
  local copies, waits for them, and re-layouts  64.2 us (14%)
  matrix products  54.9 us (12%)
  between operations  19.9 us (4%)
  other arithmetic  14.5 us (3%)
  blocking collectives  12 us (3%)
  starting transfers between devices  11.5 us (2%)
    psum x1, waiting for transfers between devices, local(): lax.psum(key_weight_local.astype(jnp.bfloat16), ('dp', 'seq'))  117 us
    reduce_scatter x1, waiting for transfers between devices, local(): lax.psum_scatter(jnp.stack(value_list).astype(jnp.bfloat16), 'seq', scatt...  64.9 us
    reduce_scatter x1, waiting for transfers between devices, local(): lax.psum_scatter(jnp.stack(key_list).astype(jnp.bfloat16), 'seq', scatter...  47.1 us
    all_gather x1, waiting for transfers between devices, local(): lax.all_gather(own_values, 'seq', axis=1, tiled=True)  36.1 us
    unnamed x118, local copies, waits for them, and re-layouts  32.8 us
    all_gather x1, waiting for transfers between devices, local(): lax.all_gather(own_keys, 'seq', axis=1, tiled=True)  16 us
    dot_general x8, matrix products, backward_block(): jnp.einsum('kgtj,jkd->tkgd', dscores, key_block, preferred_element_type=j...  13 us
  transfers between devices with their start and end apart: 7, of which 5 were waited for; matrix products, arithmetic and copies ran while one was open for 21% of the time, Pallas kernels for 0%

commit v1 on v0

--- a/solution.py
+++ b/solution.py
@@ -190,7 +190,7 @@
         "rd,rc->dc", flat_vision, value_flat, preferred_element_type=jnp.float32
     )
     key_weight_grad, value_weight_grad = (
-        lax.psum(key_weight_local.astype(jnp.bfloat16), ("dp", "seq")).astype(jnp.float32),
+        lax.psum(lax.psum(key_weight_local.astype(jnp.bfloat16), "seq"), "dp").astype(jnp.float32),
         lax.psum(value_weight_local.astype(jnp.bfloat16), ("dp", "seq")).astype(jnp.float32),
     )
     return (query_grad, vision_grad, key_weight_grad, value_weight_grad)

time: 460 us -> 580 us (1.26)
  waiting for transfers between devices: 281 us -> 400 us
    psum x1 -> x3, waiting for transfers between devices: 117 us -> 233 us  [the longest x1 150 us: local(): lax.psum(key_weight_local.astype(jnp.bfloat16), 'seq')]
    reduce_scatter x1, waiting for transfers between devices: 64.9 us -> 55.9 us  [local(): lax.psum_scatter(jnp.stack(value_list).astype(jnp.bfloat16), 'seq', scatt...]
  transfers between devices with their start and end apart: 7 -> 9, of which waited for: 5 -> 7; matrix products, arithmetic and copies ran while one was open for 21% -> 15% of each run, Pallas kernels for 0% -> 0%
where the time goes in v1:
time: 580 us; the launch traced here: 578 us
  waiting for transfers between devices  400 us (69%)
  local copies, waits for them, and re-layouts  63.9 us (11%)
  matrix products  54.9 us (9%)
  between operations  20.3 us (4%)
  other arithmetic  14.4 us (2%)
  blocking collectives  12.5 us (2%)
  starting transfers between devices  11.6 us (2%)
    psum x1, waiting for transfers between devices, local(): lax.psum(key_weight_local.astype(jnp.bfloat16), 'seq')  150 us
    psum x1, waiting for transfers between devices, local(): lax.psum(value_weight_local.astype(jnp.bfloat16), ('dp', 'seq'))  61.2 us
    reduce_scatter x1, waiting for transfers between devices, local(): lax.psum_scatter(jnp.stack(value_list).astype(jnp.bfloat16), 'seq', scatt...  55.9 us
    reduce_scatter x1, waiting for transfers between devices, local(): lax.psum_scatter(jnp.stack(key_list).astype(jnp.bfloat16), 'seq', scatter...  52.8 us
    all_gather x1, waiting for transfers between devices, local(): lax.all_gather(own_values, 'seq', axis=1, tiled=True)  36.1 us
    unnamed x118, local copies, waits for them, and re-layouts  32.7 us
    psum x1, waiting for transfers between devices, local(): lax.psum(lax.psum(key_weight_local.astype(jnp.bfloat16), 'seq'), 'dp')  22.7 us
    all_gather x1, waiting for transfers between devices, local(): lax.all_gather(own_keys, 'seq', axis=1, tiled=True)  21.6 us
  transfers between devices with their start and end apart: 9, of which 7 were waited for; matrix products, arithmetic and copies ran while one was open for 15% of the time, Pallas kernels for 0%

profile of v1, /device:TPU:0, one launch (start us, length us, event | category | flops | bytes accessed | tf_op | source)
XLA Modules:
  0.0 577.6 jit_solution(7737172217815646785)
XLA Ops:
  7.2 6.4 %copy.174 = bf16[512,4096]{1,0:T(8,128)(2,1)} copy(bf16[512,4096]{0,1:T(8,128)(2,1)} %bitcast.564) | data formatting | bytes 8388608 | tf_op jit(solution)/shard_map/dot_general | solution.py:115
  13.6 3.9 multiply_reduce_fusion.2
  18.5 3.0 convolution_convert_fusion.2
  28.1 1.6 copy.74
  29.8 2.5 fusion.117
  32.3 2.1 copy.175
  35.4 1.6 multiply_reduce_fusion
  37.0 3.0 copy.77
  40.0 2.1 multiply_convert_fusion
  42.1 21.6 %all-gather.3.cloned.1.call-done = bf16[2,640,4,128]{3,1,2,0:T(8,128)(2,1)} async-done(((bf16[2,80,4,128]{3,1,2,0:T(8,128)(2,1)}), bf16[2,640,4,128]{3,1,2,0:T(8,128)(2,1)}) %all-gather.3.cloned.1.call-update) | async-done | bytes 1310736 | tf_op jit(solution)/shard_map/all_gather | solution.py:124
  63.7 1.3 select_reduce_fusion
  65.0 1.5 select_reduce_fusion.1
  66.5 1.5 select_reduce_fusion.2
  68.0 1.5 select_reduce_fusion.3
  71.5 36.1 %all-gather.5.cloned.1.call-done = bf16[2,640,4,128]{3,1,2,0:T(8,128)(2,1)} async-done(((bf16[2,80,4,128]{3,1,2,0:T(8,128)(2,1)}), bf16[2,640,4,128]{3,1,2,0:T(8,128)(2,1)}) %all-gather.5.cloned.1.call-update) | async-done | bytes 1310736 | tf_op jit(solution)/shard_map/all_gather | solution.py:125
  107.5 1.9 fusion.94
  127.5 1.2 pad_maximum_fusion
  129.7 1.8 convolution_bitcast_fusion.23
  138.6 1.2 pad_maximum_fusion.1
  139.9 52.8 %reduce-scatter.3.cloned.1.call-done = bf16[2,80,4,128]{3,1,2,0:T(8,128)(2,1)} async-done(((bf16[2,640,4,128]{3,1,2,0:T(8,128)(2,1)}), bf16[2,80,4,128]{3,1,2,0:T(8,128)(2,1)}) %reduce-scatter.3.cloned.1.call-update) | async-done | bytes 163856 | tf_op jit(solution)/shard_map/reduce_scatter | solution.py:149
  195.8 3.3 fusion
  199.1 5.6 all-to-all-start.1
  204.8 55.9 %reduce-scatter.5.cloned.1.call-done = bf16[2,80,4,128]{3,1,2,0:T(8,128)(2,1)} async-done(((bf16[2,640,4,128]{3,1,2,0:T(8,128)(2,1)}), bf16[2,80,4,128]{3,1,2,0:T(8,128)(2,1)}) %reduce-scatter.5.cloned.1.call-update) | async-done | bytes 163856 | tf_op jit(solution)/shard_map/reduce_scatter | solution.py:152
  261.7 3.2 fusion.1
  265.0 5.7 all-to-all-start
  270.7 149.5 %all-reduce.8.cloned.1.call-done = bf16[4096,512]{0,1:T(8,128)(2,1)} async-done(((bf16[4096,512]{0,1:T(8,128)(2,1)}), bf16[4096,512]{0,1:T(8,128)(2,1)}) %all-reduce.8.cloned.1.call-update) | async-done | bytes 4194320 | tf_op jit(solution)/shard_map/psum | solution.py:193
  420.3 6.5 %copy.111 = bf16[2048,2,512]{0,2,1:T(8,128)(2,1)} copy(bf16[2048,2,512]{2,0,1:T(8,128)(2,1)} %bitcast.180) | data formatting | bytes 8388608 | tf_op jit(solution)/shard_map/all_to_all | solution.py:168
  426.7 6.2 %copy.101 = bf16[2048,2,512]{0,2,1:T(8,128)(2,1)} copy(bf16[2048,2,512]{2,0,1:T(8,128)(2,1)} %bitcast.145) | data formatting | bytes 8388608 | tf_op jit(solution)/shard_map/all_to_all | solution.py:167
  432.9 1.5 fusion.110
  434.4 1.5 convolution_add_fusion.3
  436.0 1.5 convolution_add_fusion.2
  437.5 1.5 fusion.32
  439.0 1.3 copy.98
  440.6 1.5 fusion.109
  442.1 1.5 convolution_add_fusion.9
  443.7 1.5 convolution_add_fusion.8
  445.2 2.5 fusion.33
  447.7 2.7 copy.88
  450.4 2.3 fusion.7
  453.6 1.3 copy.114
  454.9 6.5 %all_gather.15 = bf16[2,80,8,128]{3,1,2,0:T(8,128)(2,1)S(1)} all-gather(bf16[2,80,4,128]{3,1,2,0:T(8,128)(2,1)S(1)} %copy-done.31), channel_id=1, replica_groups=mesh['dp'=2,'seq'=8,'mp'=2] {'mp'}, dimensions={2}, use_global_device_ids=true | all-gather | bytes 491520 | tf_op jit(solution)/shard_map/all_gather | solution.py:164
  461.5 6.0 %all_gather.14 = bf16[2,80,8,128]{3,1,2,0:T(8,128)(2,1)S(1)} all-gather(bf16[2,80,4,128]{3,1,2,0:T(8,128)(2,1)S(1)} %copy-done.28), channel_id=1, replica_groups=mesh['dp'=2,'seq'=8,'mp'=2] {'mp'}, dimensions={2}, use_global_device_ids=true | all-gather | bytes 491520 | tf_op jit(solution)/shard_map/all_gather | solution.py:163
  467.6 3.2 fusion.84
  471.1 1.7 fusion.2
  472.8 61.2 %all-reduce.12.cloned.1.call-done = bf16[4096,512]{0,1:T(8,128)(2,1)} async-done(((bf16[4096,512]{0,1:T(8,128)(2,1)}), bf16[4096,512]{0,1:T(8,128)(2,1)}) %all-reduce.12.cloned.1.call-update) | async-done | bytes 4194320 | tf_op jit(solution)/shard_map/psum | solution.py:194
  533.9 7.0 %copy.116 = f32[4096,512]{1,0:T(8,128)} copy(bf16[4096,512]{0,1:T(8,128)(2,1)} %all-reduce.12.cloned.1.call-done) | data formatting | bytes 12582912
  541.0 22.7 %all-reduce.10.cloned.1.call-done = bf16[4096,512]{0,1:T(8,128)(2,1)} async-done(((bf16[4096,512]{0,1:T(8,128)(2,1)}), bf16[4096,512]{0,1:T(8,128)(2,1)}) %all-reduce.10.cloned.1.call-update) | async-done | bytes 4194320 | tf_op jit(solution)/shard_map/psum | solution.py:193
  563.7 7.0 %copy.115 = f32[4096,512]{1,0:T(8,128)} copy(bf16[4096,512]{0,1:T(8,128)(2,1)} %all-reduce.10.cloned.1.call-done) | data formatting | bytes 12582912
  (191 shorter events, 36.8 us)
Async XLA Ops:
  7.2 6.5 %copy-start = (bf16[2,80,4096]{2,1,0:T(8,128)(2,1)S(1)}, bf16[2,80,4096]{2,1,0:T(8,128)(2,1)}, u32[]{:S(2)}) copy-start(bf16[2,80,4096]{2,1,0:T(8,128)(2,1)} %param.41) | copy-start | bytes 3932164
  7.2 56.5 %all-gather.3.cloned.1.call-start = ((), (), s32[]{:S(2)}) async-start(), calls=%async_computation.4 | async-start | bytes 1474560 | tf_op jit(solution)/shard_map/all_gather | solution.py:124
  13.6 3.9 copy-start.51
  18.4 89.1 %all-gather.5.cloned.1.call-start = ((), (), s32[]{:S(2)}) async-start(), calls=%async_computation.5 | async-start | bytes 1474560 | tf_op jit(solution)/shard_map/all_gather | solution.py:125
  18.5 3.9 copy-start.54
  22.3 170.4 %reduce-scatter.3.cloned.1.call-start = ((), (), s32[]{:S(2)}) async-start(), calls=%async_computation.6 | async-start | bytes 1474560 | tf_op jit(solution)/shard_map/reduce_scatter | solution.py:149
  29.8 5.6 copy-start.3
  37.0 3.0 copy-start.52
  65.0 5.0 copy-start.7
  66.5 3.5 copy-start.10
  68.0 2.1 copy-start.13
  107.5 2.0 copy-start.14
  107.5 2.2 copy-start.55
  112.3 1.4 copy-start.47
  114.2 1.3 copy-start.6
  115.9 10.2 %copy-start.16 = (f32[4,4,128,160]{2,3,1,0:T(8,128)}, f32[4,4,128,160]{2,3,1,0:T(8,128)S(1)}, u32[]{:S(2)}) copy-start(f32[4,4,128,160]{2,3,1,0:T(8,128)S(1)} %get-tuple-element.233) | copy-start | bytes 3932164
  116.3 8.9 %copy-start.18 = (f32[4,4,128,160]{2,3,1,0:T(8,128)}, f32[4,4,128,160]{2,3,1,0:T(8,128)S(1)}, u32[]{:S(2)}) copy-start(f32[4,4,128,160]{2,3,1,0:T(8,128)S(1)} %get-tuple-element.235) | copy-start | bytes 3932164
  116.7 7.4 %copy-start.20 = (f32[4,4,128,160]{2,3,1,0:T(8,128)}, f32[4,4,128,160]{2,3,1,0:T(8,128)S(1)}, u32[]{:S(2)}) copy-start(f32[4,4,128,160]{2,3,1,0:T(8,128)S(1)} %get-tuple-element.237) | copy-start | bytes 3932164
  117.0 3.5 copy-start.22
  118.2 8.0 %copy-start.49 = (f32[4,4,128]{2,1,0:T(4,128)}, f32[4,4,128]{2,1,0:T(4,128)S(1)}, u32[]{:S(2)}) copy-start(f32[4,4,128]{2,1,0:T(4,128)S(1)} %multiply_add_fusion.1) | copy-start | bytes 24580
  128.7 132.0 %reduce-scatter.5.cloned.1.call-start = ((), (), s32[]{:S(2)}) async-start(), calls=%async_computation.7 | async-start | bytes 1474560 | tf_op jit(solution)/shard_map/reduce_scatter | solution.py:152
  129.7 1.9 copy-start.15
  129.7 1.9 copy-start.48
  131.6 1.3 copy-start.12
  134.3 1.3 copy-start.21
  134.3 1.3 copy-start.50
  135.6 1.3 copy-start.19
  139.8 280.4 %all-reduce.8.cloned.1.call-start = ((), (), s32[]{:S(2)}) async-start(), calls=%async_computation.8 | async-start | bytes 8388608 | tf_op jit(solution)/shard_map/psum | solution.py:193
  199.1 65.8 %all-to-all-start.1 = ((bf16[2,2048,512]{2,1,0:T(8,128)(2,1)}), bf16[2,2048,512]{2,1,0:T(8,128)(2,1)}, u32[]{:S(2)}, u32[]{:S(2)}) async-start(bf16[2,2048,512]{2,1,0:T(8,128)(2,1)} %bitcast.563), calls=%async_computation.3 | async-start | bytes 8388608 | tf_op jit(solution)/shard_map/all_to_all | solution.py:168
  204.7 329.2 %all-reduce.12.cloned.1.call-start = ((), (), s32[]{:S(2)}) async-start(), calls=%async_computation.10 | async-start | bytes 8388608 | tf_op jit(solution)/shard_map/psum | solution.py:194
  265.0 161.8 %all-to-all-start = ((bf16[2,2048,512]{2,1,0:T(8,128)(2,1)}), bf16[2,2048,512]{2,1,0:T(8,128)(2,1)}, u32[]{:S(2)}, u32[]{:S(2)}) async-start(bf16[2,2048,512]{2,1,0:T(8,128)(2,1)} %bitcast.565), calls=%async_computation.1 | async-start | bytes 8388608 | tf_op jit(solution)/shard_map/all_to_all | solution.py:167
  270.6 293.0 %all-reduce.10.cloned.1.call-start = ((), (), s32[]{:S(2)}) async-start(), calls=%async_computation.9 | async-start | bytes 8388608 | tf_op jit(solution)/shard_map/psum | solution.py:193
  432.9 1.5 copy-start.39
  434.4 1.5 copy-start.41
  436.0 1.5 copy-start.43
  439.0 3.1 copy-start.5
  439.0 1.6 copy-start.30
  440.6 1.5 copy-start.35
  442.1 1.5 copy-start.37
  443.6 1.5 copy-start.33
  447.7 2.7 copy-start.1
  447.7 2.7 copy-start.53
  450.4 2.4 copy-start.4
  450.4 2.4 copy-start.25
  450.4 2.5 copy-start.26
  453.5 1.3 copy-start.31
  453.6 7.9 %copy-start.28 = (bf16[2,80,4,128]{3,1,2,0:T(8,128)(2,1)S(1)}, bf16[2,80,4,128]{3,1,2,0:T(8,128)(2,1)}, u32[]{:S(2)}) copy-start(bf16[2,80,4,128]{3,1,2,0:T(8,128)(2,1)} %copy-done.27) | copy-start | bytes 491524
  467.6 3.5 copy-start.2
  (17 other events, 18.0 us)
Sparse Core Ops, SparseCore 0:
  18.6 45.1 all-gather.2
  66.5 40.9 all-gather.4
  128.8 63.8 reduce-scatter.2
  196.5 64.1 reduce-scatter.4
  264.8 155.3 all-reduce.7
  423.8 110.1 all-reduce.11
  536.4 27.1 all-reduce.9
